TPU v7x, 16 devices: a whole 2x2x2 slice. The times are simulated.
16 devices in a mesh: tp: 2 (over z), cp: 8 (over y, x, core).
Axes of the slice: x: 2, y: 2, z: 2, core: 2. Of those that a mesh axis runs over, the one named last changes fastest.
Arguments:
- x_in: bfloat16 [32, 2048, 1024], P(None, 'cp')
- grad_z: bfloat16 [32, 2048, 1024], P(None, 'cp')
- seg_pos: int32 [32, 2048], P(None, 'cp')
- norm_scale: bfloat16 [1024], replicated
- w_x: bfloat16 [1024, 1024], P(None, 'tp')
- b_x: bfloat16 [1024], P('tp')
- w_y: bfloat16 [1024, 1024], P(None, 'tp')
- b_y: bfloat16 [1024], P('tp')
- conv_w: bfloat16 [4, 1024], P(None, 'tp')
- conv_b: bfloat16 [1024], P('tp')
- w_a: bfloat16 [8, 128, 128], P('tp')
- b_a: bfloat16 [1024], P('tp')
- w_i: bfloat16 [8, 128, 128], P('tp')
- b_i: bfloat16 [1024], P('tp')
- a_param: float32 [1024], P('tp')
- w_out: bfloat16 [1024, 1024], P('tp')
- b_out: bfloat16 [1024], replicated
Outputs:
- output 1: bfloat16 [32, 2048, 1024], P(None, 'cp')
- output 2: bfloat16 [32, 2048, 1024], P(None, 'cp')
- output 3: float32 [1024], replicated
- output 4: float32 [1024, 1024], P(None, 'tp')
- output 5: float32 [1024], P('tp')
- output 6: float32 [1024, 1024], P(None, 'tp')
- output 7: float32 [1024], P('tp')
- output 8: float32 [4, 1024], P(None, 'tp')
- output 9: float32 [1024], P('tp')
- output 10: float32 [8, 128, 128], P('tp')
- output 11: float32 [1024], P('tp')
- output 12: float32 [8, 128, 128], P('tp')
- output 13: float32 [1024], P('tp')
- output 14: float32 [1024], P('tp')
- output 15: float32 [1024, 1024], P('tp')
- output 16: float32 [1024], replicated
All inputs are finite; a program needn't handle non-finite values.
Results may differ from a plain program's by a relative error of at most 0.00761529.
Values sent between devices are 32-bit elements.
A program may use at most 1 GiB of HBM per device.

v0:
```python
import functools
import jax
import jax.numpy as jnp
from jax import lax
from jax.sharding import PartitionSpec as P

NORM_EPS = 1e-6
CONV_WIDTH = 4
BORROW_ROWS = CONV_WIDTH - 1
IN_SPECS = (P(None, "cp", None), P(None, "cp", None), P(None, "cp"), P(), P(None, "tp"), P("tp"), P(None, "tp"), P("tp"), P(None, "tp"), P("tp"), P("tp", None, None), P("tp"), P("tp", None, None), P("tp"), P("tp"), P("tp", None), P())
OUT_SPECS = (P(None, "cp", None), P(None, "cp", None), P(), P(None, "tp"), P("tp"), P(None, "tp"), P("tp"), P(None, "tp"), P("tp"), P("tp", None, None), P("tp"), P("tp", None, None), P("tp"), P("tp"), P("tp", None), P())


def norm_apply(x_f, scale_f):
    mean_sq = jnp.mean(x_f * x_f, axis=-1, keepdims=True)
    return x_f * lax.rsqrt(mean_sq + NORM_EPS) * (1.0 + scale_f)


def gelu_tanh(pre_y):
    return jax.nn.gelu(pre_y, approximate=True)


def gate_math(pre_a, pre_i, conv_f, a_param, reset_mask):
    log_a = -8.0 * jax.nn.sigmoid(pre_a) * jax.nn.softplus(a_param)
    decays = jnp.where(reset_mask, 0.0, jnp.exp(log_a))
    multiplier = jnp.where(reset_mask, 1.0, jnp.sqrt(-jnp.expm1(2.0 * log_a)))
    return decays, multiplier * jax.nn.sigmoid(pre_i) * conv_f


def conv_apply(xb_ext, conv_w, conv_b, pos_t):
    n_rows = pos_t.shape[0]
    conv_wf = conv_w.astype(jnp.float32)
    conv_sum = conv_b.astype(jnp.float32)
    for tap_k in range(CONV_WIDTH):
        start_row = BORROW_ROWS - tap_k
        keep_mask = (pos_t >= tap_k)[:, :, None]
        conv_sum = conv_sum + jnp.where(keep_mask, xb_ext[start_row:start_row + n_rows], 0.0) * conv_wf[tap_k]
    return conv_sum


def conv_back(grad_conv, xb_ext, conv_w, pos_t):
    n_rows = pos_t.shape[0]
    conv_wf = conv_w.astype(jnp.float32)
    grad_ext = 0.0
    tap_grads = []
    for tap_k in range(CONV_WIDTH):
        start_row = BORROW_ROWS - tap_k
        masked = jnp.where((pos_t >= tap_k)[:, :, None], grad_conv, 0.0)
        tap_grads.append(jnp.sum(masked * xb_ext[start_row:start_row + n_rows], axis=(0, 1)))
        grad_ext = grad_ext + jnp.pad(masked * conv_wf[tap_k], ((start_row, tap_k), (0, 0), (0, 0)))
    return grad_ext, jnp.stack(tap_grads), jnp.sum(grad_conv, axis=(0, 1))


def local_scan(decays, drives):
    def scan_step(carry_in, inputs_t):
        state_h, prod_a = carry_in
        state_h = inputs_t[0] * state_h + inputs_t[1]
        prod_a = inputs_t[0] * prod_a
        return (state_h, prod_a), (state_h, prod_a)
    zeros_h = jnp.zeros(decays.shape[1:], jnp.float32)
    _, (states, run_prods) = lax.scan(scan_step, (zeros_h, jnp.ones_like(zeros_h)), (decays, drives))
    return states, run_prods


def local_scan_back(decays, grad_out):
    def scan_step(carry_in, inputs_t):
        next_grad, prod_a = carry_in
        grad_h = inputs_t[1] + next_grad
        return (inputs_t[0] * grad_h, inputs_t[0] * prod_a), (grad_h, prod_a)
    zeros_h = jnp.zeros(decays.shape[1:], jnp.float32)
    (head_grad, total_prod), (grad_loc, suffix_prods) = lax.scan(scan_step, (zeros_h, jnp.ones_like(zeros_h)), (decays, grad_out), reverse=True)
    return grad_loc, suffix_prods, head_grad, total_prod


def carry_in_forward(end_info, cp_index):
    def compose(carry_in, piece_info):
        return piece_info[0] * carry_in + piece_info[1], carry_in
    _, entering = lax.scan(compose, jnp.zeros_like(end_info[0, 0]), end_info)
    return lax.dynamic_index_in_dim(entering, cp_index, 0, keepdims=False)


def carry_in_backward(head_info, cp_index):
    def compose(carry_in, piece_info):
        return piece_info[0] * carry_in + piece_info[1], carry_in
    _, entering = lax.scan(compose, jnp.zeros_like(head_info[0, 0]), head_info, reverse=True)
    return lax.dynamic_index_in_dim(entering, cp_index, 0, keepdims=False)


def shard_body(x_in, grad_z, seg_pos, norm_scale, w_x, b_x, w_y, b_y, conv_w, conv_b, w_a, b_a, w_i, b_i, a_param, w_out, b_out, fwd_perm, back_perm):
    cp_index = lax.axis_index("cp")
    n_tok = x_in.shape[1]
    n_blocks, blk_width = w_a.shape[0], w_a.shape[1]
    x_f = x_in.astype(jnp.float32)
    normed_f, norm_pull = jax.vjp(norm_apply, x_f, norm_scale.astype(jnp.float32))
    normed = normed_f.astype(jnp.bfloat16)
    pre_y = jnp.einsum("btd,dl->tbl", normed, w_y, preferred_element_type=jnp.float32) + b_y
    y_act, gelu_pull = jax.vjp(gelu_tanh, pre_y)
    x_branch = (jnp.einsum("btd,dl->tbl", normed, w_x, preferred_element_type=jnp.float32) + b_x).astype(jnp.bfloat16).astype(jnp.float32)
    borrowed = lax.ppermute(x_branch[n_tok - BORROW_ROWS:], "cp", fwd_perm)
    xb_ext = jnp.concatenate([borrowed, x_branch], axis=0)
    pos_t = seg_pos.T
    conv_out = conv_apply(xb_ext, conv_w, conv_b, pos_t).astype(jnp.bfloat16)
    blocks = conv_out.reshape(conv_out.shape[0], conv_out.shape[1], n_blocks, blk_width)
    pre_a = jnp.einsum("tbhk,hkj->tbhj", blocks, w_a, preferred_element_type=jnp.float32).reshape(conv_out.shape) + b_a
    pre_i = jnp.einsum("tbhk,hkj->tbhj", blocks, w_i, preferred_element_type=jnp.float32).reshape(conv_out.shape) + b_i
    gate_fn = functools.partial(gate_math, reset_mask=(pos_t == 0)[:, :, None])
    (decays, drives), gate_pull = jax.vjp(gate_fn, pre_a, pre_i, conv_out.astype(jnp.float32), a_param)
    states, run_prods = local_scan(decays, drives)
    end_info = lax.all_gather(jnp.stack([run_prods[-1], states[-1]]), "cp")
    state_in = carry_in_forward(end_info, cp_index)
    hidden = states + run_prods * state_in
    prev_hidden = jnp.concatenate([state_in[None], hidden[:-1]], axis=0)
    mixed_v = (hidden * y_act).astype(jnp.bfloat16)
    out_part = jnp.einsum("tbl,ld->btd", mixed_v, w_out, preferred_element_type=jnp.float32)
    out_proj = lax.psum(out_part, "tp") + b_out
    z_out = (x_f + out_proj).astype(jnp.bfloat16)

    d_mixed = jnp.einsum("btd,ld->tbl", grad_z, w_out, preferred_element_type=jnp.float32)
    g_w_out = jnp.einsum("tbl,btd->ld", mixed_v, grad_z, preferred_element_type=jnp.float32)
    g_b_out = jnp.sum(grad_z, axis=(0, 1), dtype=jnp.float32)
    d_pre_y = gelu_pull(d_mixed * hidden)[0]
    grad_loc, suffix_prods, head_grad, total_prod = local_scan_back(decays, d_mixed * y_act)
    head_info = lax.all_gather(jnp.stack([total_prod, head_grad]), "cp")
    grad_in = carry_in_backward(head_info, cp_index)
    d_hidden = grad_loc + suffix_prods * grad_in
    d_pre_a, d_pre_i, d_conv_f, g_a_param = gate_pull((d_hidden * prev_hidden, d_hidden))
    d_pre_a16 = d_pre_a.astype(jnp.bfloat16).reshape(blocks.shape)
    d_pre_i16 = d_pre_i.astype(jnp.bfloat16).reshape(blocks.shape)
    g_w_a = jnp.einsum("tbhk,tbhj->hkj", blocks, d_pre_a16, preferred_element_type=jnp.float32)
    g_w_i = jnp.einsum("tbhk,tbhj->hkj", blocks, d_pre_i16, preferred_element_type=jnp.float32)
    d_gate_in = jnp.einsum("tbhj,hkj->tbhk", d_pre_a16, w_a, preferred_element_type=jnp.float32) + jnp.einsum("tbhj,hkj->tbhk", d_pre_i16, w_i, preferred_element_type=jnp.float32)
    d_conv = d_conv_f + d_gate_in.reshape(conv_out.shape)
    grad_ext, g_conv_w, g_conv_b = conv_back(d_conv, xb_ext, conv_w, pos_t)
    returned = lax.ppermute(grad_ext[:BORROW_ROWS], "cp", back_perm)
    d_branch = jnp.concatenate([grad_ext[BORROW_ROWS:n_tok], grad_ext[n_tok:] + returned], axis=0)
    d_branch16 = d_branch.astype(jnp.bfloat16)
    d_pre_y16 = d_pre_y.astype(jnp.bfloat16)
    g_w_x = jnp.einsum("btd,tbl->dl", normed, d_branch16, preferred_element_type=jnp.float32)
    g_w_y = jnp.einsum("btd,tbl->dl", normed, d_pre_y16, preferred_element_type=jnp.float32)
    d_norm_part = jnp.einsum("tbl,dl->btd", d_branch16, w_x, preferred_element_type=jnp.float32) + jnp.einsum("tbl,dl->btd", d_pre_y16, w_y, preferred_element_type=jnp.float32)
    d_normed = lax.psum(d_norm_part, "tp")
    d_x_norm, g_scale = norm_pull(d_normed)
    grad_x = (grad_z.astype(jnp.float32) + d_x_norm).astype(jnp.bfloat16)
    grad_sums = lax.psum((g_scale, g_w_x, jnp.sum(d_branch, axis=(0, 1)), g_w_y, jnp.sum(d_pre_y, axis=(0, 1)), g_conv_w, g_conv_b, g_w_a, jnp.sum(d_pre_a, axis=(0, 1)), g_w_i, jnp.sum(d_pre_i, axis=(0, 1)), g_a_param, g_w_out, g_b_out), "cp")
    return (z_out, grad_x) + tuple(grad_sums)


def solution(mesh):
    cp_size = mesh.shape["cp"]
    fwd_perm = [(dev_j, dev_j + 1) for dev_j in range(cp_size - 1)]
    back_perm = [(dev_j + 1, dev_j) for dev_j in range(cp_size - 1)]
    per_device = functools.partial(shard_body, fwd_perm=fwd_perm, back_perm=back_perm)
    return jax.shard_map(per_device, mesh=mesh, in_specs=IN_SPECS, out_specs=OUT_SPECS, check_vma=False)
```

profile of v0, /device:TPU:0, one launch (start us, length us, event | category | flops | bytes accessed | tf_op | source)
XLA Modules:
  0.0 4627.9 jit_solution(543501514195676246)
XLA Ops:
  51.6 28.0 bitcast_multiply_fusion.5
  80.3 28.5 add_convert_fusion
  146.5 19.2 copy.64
  165.6 20.3 reshape.98
  197.0 20.1 copy.70
  232.9 1636.1 %while.70 = (s32[]{:T(128)}, f32[32,512]{1,0:T(8,128)S(1)}, f32[32,512]{1,0:T(8,128)S(1)}, f32[256,32,512]{2,0,1:T(8,128)}, f32[256,32,512]{2,0,1:T(8,128)}, /*i...) while((s32[]{:T(128)}, f32[32,512]{1,0:T(8,128)S(1)}, ...), condition=%wide.region_7.8_spmd.clone, body=%wide.region_6.7_spmd.clone.sunk | while | flops 81924 | bytes 1179787 | solution.py:71
  1881.4 19.4 copy.67
  1900.8 19.9 reshape.99
  1928.4 44.5 fusion.86
  1972.9 675.7 %while.68 = (s32[]{:T(128)}, f32[32,512]{1,0:T(8,128)S(1)}, f32[32,512]{1,0:T(8,128)S(1)}, f32[256,32,512]{2,1,0:T(8,128)}, f32[256,32,512]{2,1,0:T(8,128)}, /*i...) while((s32[]{:T(128)}, f32[32,512]{1,0:T(8,128)S(1)}, ...), condition=%wide.region_2.3_spmd.clone, body=%wide.region_1.2_spmd.clone.sunk | while | flops 81923 | bytes 655979 | solution.py:61
  2651.0 21.8 all-gather.5.cloned.1.call-done
  2685.8 40.2 fusion.89
  2741.6 39.2 multiply_reduce_fusion
  2843.2 19.9 reshape.102
  2863.2 49.1 %multiply_reduce_fusion.3 = (f32[512]{0:T(512)}, f32[512]{0:T(512)}, f32[512]{0:T(512)}, f32[512]{0:T(512)}, f32[512]{0:T(512)}, /*index=5*/f32[256,32,512]{2,0,1:T(8,128)}) fusion(pred[256,32]{0,1:T(8,128)(4,1)S(1)} %copy-done.15, f32[256,32,512]{2,0,1:T(8,128)} %convert_bitcast_fusion, f32[3,32,512]{2,0,1:T(4,128)S(1)} %copy-done.4, ...), kind=kLoop, calls=%fused_computation.77 | loop fusion | flops 130020864 | bytes 100917248 | tf_op jit(solution)/shard_map/reduce_sum | solution.py:49
  2912.3 26.1 select_multiply_fusion.3
  2942.2 19.3 fusion.51
  2977.2 29.0 pad_add_fusion
  3017.7 26.0 add_bitcast_fusion
  3121.4 1377.8 %all-reduce.12.cloned.1.call-done = (f32[32,256,1024]{2,1,0:T(8,128)}, f32[32,256,1024]{2,1,0:T(8,128)}) async-done(((f32[32,256,1024]{2,1,0:T(8,128)}, f32[32,256,1024]{2,1,0:T(8,128)}), (f32[32,256,1024]{2,1,0:T(8,128)}, f32[32,256,1024]{2,1,0:T(8,128)})) %all-reduce.12.cloned.1.call-update) | async-done | bytes 67108880 | tf_op jit(solution)/shard_map/psum | solution.py:115
  4499.1 19.5 fusion.10
  4518.8 44.3 convert_reduce_fusion
  4563.0 25.0 all-reduce.4
  4588.1 20.4 all-reduce.10.cloned.1.call-done
  (2280 shorter events, 2667.5 us)
Async XLA Ops:
  7.2 44.4 copy-start
  7.2 1913.5 %all-gather.7.cloned.1.call-start = ((), (), s32[]{:S(2)}) async-start(), calls=%async_computation.1 | async-start | bytes 1179648 | tf_op jit(solution)/shard_map/all_gather | solution.py:123
  32.5 47.7 %collective-permute-start = (f32[3,32,512]{2,0,1:T(4,128)S(1)}, f32[3,32,512]{2,0,1:T(4,128)S(1)}, u32[]{:S(2)}, u32[]{:S(2)}) collective-permute-start(f32[3,32,512]{2,0,1:T(4,128)S(1)} %slice.96), channel_id=1, source_target_pairs={{0,1},{1,2},{2,3},{3,4},{4,5},{5,6},{6,7},{8,9},{9,10},{10,11},{11... | collective-permute-start | bytes 589832 | tf_op jit(solution)/shard_map/ppermute | solution.py:99
  35.4 44.8 copy-start.12
  35.4 44.8 copy-start.14
  35.4 44.8 copy-start.16
  35.4 44.8 copy-start.18
  35.5 44.8 copy-start.23
  35.5 44.8 copy-start.25
  35.5 44.8 copy-start.27
  35.5 44.8 copy-start.29
  217.1 1652.7 %copy-start.50 = (bf16[512]{0:T(512)(128)(2,1)S(1)}, bf16[512]{0:T(512)(128)(2,1)}, u32[]{:S(2)}) copy-start(bf16[512]{0:T(512)(128)(2,1)} %param.38) | copy-start | bytes 3076
  217.1 1652.7 %copy-start.7 = (bf16[4,128,128]{2,1,0:T(8,128)(2,1)S(1)}, bf16[4,128,128]{2,1,0:T(8,128)(2,1)}, u32[]{:S(2)}) copy-start(bf16[4,128,128]{2,1,0:T(8,128)(2,1)} %param.37) | copy-start | bytes 393220
  1869.7 803.2 %all-gather.5.cloned.1.call-start = ((), (), s32[]{:S(2)}) async-start(), calls=%async_computation | async-start | bytes 1179648 | tf_op jit(solution)/shard_map/all_gather | solution.py:109
  2651.0 1848.2 %all-reduce.12.cloned.1.call-start = ((), (), s32[]{:S(2)}) async-start(), calls=%async_computation.3 | async-start | bytes 134217728 | tf_op jit(solution)/shard_map/psum | solution.py:115
  2863.2 49.1 %copy-start.24 = (f32[1,512]{1,0:T(1,128)S(1)}, f32[1,512]{1,0:T(1,128)}, u32[]{:S(2)}) copy-start(f32[1,512]{1,0:T(1,128)} %copy-done.23) | copy-start | bytes 6148
  2863.2 49.1 %copy-start.26 = (f32[1,512]{1,0:T(1,128)S(1)}, f32[1,512]{1,0:T(1,128)}, u32[]{:S(2)}) copy-start(f32[1,512]{1,0:T(1,128)} %copy-done.25) | copy-start | bytes 6148
  2863.2 49.1 %copy-start.28 = (f32[1,512]{1,0:T(1,128)S(1)}, f32[1,512]{1,0:T(1,128)}, u32[]{:S(2)}) copy-start(f32[1,512]{1,0:T(1,128)} %copy-done.27) | copy-start | bytes 6148
  2863.2 49.1 %copy-start.30 = (f32[1,512]{1,0:T(1,128)S(1)}, f32[1,512]{1,0:T(1,128)}, u32[]{:S(2)}) copy-start(f32[1,512]{1,0:T(1,128)} %copy-done.29) | copy-start | bytes 6148
  2940.9 75.2 %collective-permute-start.1 = (f32[3,32,512]{2,0,1:T(4,128)}, f32[3,32,512]{2,0,1:T(4,128)S(1)}, u32[]{:S(2)}, u32[]{:S(2)}) collective-permute-start(f32[3,32,512]{2,0,1:T(4,128)} %pad_add_fusion.1), channel_id=1, source_target_pairs={{1,0},{2,1},{3,2},{4,3},{5,4},{6,5},{7,6},{9,8},{10,9},{11,10},{12... | collective-permute-start | bytes 589832 | tf_op jit(solution)/shard_map/ppermute | solution.py:134
  3043.9 1564.6 %all-reduce.10.cloned.1.call-start = ((), (), s32[]{:S(2)}) async-start(), calls=%async_computation.2 | async-start | bytes 13631488 | tf_op jit(solution)/shard_map/psum | solution.py:144
  4518.7 44.3 copy-start.33
  4518.7 44.3 copy-start.34
  4518.7 44.3 copy-start.39
  (38 other events, 624.5 us)
Sparse Core Ops, SparseCore 0:
  1869.8 21.7 all-gather.6
  2651.1 21.7 all-gather.4
  3043.9 1455.1 all-reduce.11
  4504.0 104.4 all-reduce.9
where the time goes:
time: 4690 us; the launch traced here: 4630 us
  local copies, waits for them, and re-layouts  1890 us (40%)
  waiting for transfers between devices  1420 us (30%)
  other arithmetic  1020 us (22%)
  matrix products  240 us (5%)
    psum x1, waiting for transfers between devices, shard_body(): out_proj = lax.psum(out_part, 'tp') + b_out  1380 us
    dynamic_update_slice x1024, local copies, waits for them, and re-layouts, local_scan(): lax.scan(scan_step, (zeros_h, jnp.ones_like(zeros_h)), (decays, drives))  1120 us
    dynamic_slice x512, local copies, waits for them, and re-layouts, local_scan(): lax.scan(scan_step, (zeros_h, jnp.ones_like(zeros_h)), (decays, drives))  559 us
    dynamic_update_slice x256, other arithmetic, local_scan(): lax.scan(scan_step, (zeros_h, jnp.ones_like(zeros_h)), (decays, drives))  394 us
    mul x256, other arithmetic, scan_step(): return ((inputs_t[0] * grad_h, inputs_t[0] * prod_a), (grad_h, prod_a))  229 us
  transfers between devices with their start and end apart: 6, of which 3 were waited for; matrix products, arithmetic and copies ran while one was open for 7% of the time, Pallas kernels for 0%

commit v1 on v0

v1 whole, which is shorter than its diff:
```python
import functools
import jax
import jax.numpy as jnp
import numpy as np
from jax import lax
from jax.experimental import pallas as pl
from jax.experimental.pallas import tpu as pltpu
from jax.sharding import PartitionSpec as P

NORM_EPS = 1e-6
CONV_WIDTH = 4
BORROW = CONV_WIDTH - 1
LANES = 128
TB = 16
TINY = 1e-37
VMEM_BYTES = 66 * 1000 * 1000
F32 = jnp.float32
BF16 = jnp.bfloat16
IN_SPECS = (P(None, "cp", None), P(None, "cp", None), P(None, "cp"), P(), P(None, "tp"), P("tp"), P(None, "tp"), P("tp"), P(None, "tp"), P("tp"), P("tp", None, None), P("tp"), P("tp", None, None), P("tp"), P("tp"), P("tp", None), P())
OUT_SPECS = (P(None, "cp", None), P(None, "cp", None), P(), P(None, "tp"), P("tp"), P(None, "tp"), P("tp"), P(None, "tp"), P("tp"), P("tp", None, None), P("tp"), P("tp", None, None), P("tp"), P("tp"), P("tp", None), P())
V_BX, V_BY, V_CW, V_CB, V_BA, V_BI, V_SP = 0, 1, 2, 6, 7, 8, 9
S_BX, S_BY, S_CW, S_CB, S_BA, S_BI, S_AP = 0, 1, 2, 6, 7, 8, 9
LOG2E = 1.4426950408889634
RESET_LOG = -1e4
GELU_C = 0.7978845608028654
GELU_D = 0.044715


def dot_nn(lhs, rhs):
    return lax.dot_general(lhs, rhs, (((1,), (0,)), ((), ())), preferred_element_type=F32)


def dot_nt(lhs, rhs):
    return lax.dot_general(lhs, rhs, (((1,), (1,)), ((), ())), preferred_element_type=F32)


def dot_tn(lhs, rhs):
    return lax.dot_general(lhs, rhs, (((0,), (0,)), ((), ())), preferred_element_type=F32)


def sigm_scaled(val, bias):
    root = lax.rsqrt(1.0 + jnp.exp2(val * (-LOG2E) + bias))
    return root * root


def fold8(val):
    return (val[0:8] + val[8:16]) + (val[16:24] + val[24:32])


def to_time_major(perm, src_ref, dst_ref):
    n_seq, _, width = src_ref.shape
    for h in range(n_seq // TB):
        rows = src_ref[h * TB:(h + 1) * TB].reshape(TB * TB, width)
        dst_ref[:, h * TB:(h + 1) * TB, :] = dot_nn(perm, rows).astype(BF16).reshape(TB, TB, width)


def to_batch_major(perm, src_ref, dst_ref):
    n_seq, width = src_ref.shape[1], src_ref.shape[2]
    for h in range(n_seq // TB):
        rows = src_ref[:, h * TB:(h + 1) * TB, :].reshape(TB * TB, width)
        dst_ref[h * TB:(h + 1) * TB] = dot_nn(perm, rows).astype(BF16).reshape(TB, TB, width)


def norm_rows(xf, gain):
    rs = lax.rsqrt(jnp.mean(xf * xf, axis=-1, keepdims=True) + NORM_EPS)
    return (xf * rs * gain).astype(BF16)


def chunk_vec(vec_ref, col):
    return lambda row: vec_ref[row:row + 1, col]


def gate_terms(pa, pi, vec, cap):
    r = sigm_scaled(pa, vec(V_BA))
    i = sigm_scaled(pi, vec(V_BI))
    log_a = jnp.minimum(vec(V_SP) * r, cap)
    a = jnp.exp(log_a)
    a2 = a * a
    m2 = jnp.tanh(log_a) * (-1.0 - a2)
    inv_m = lax.rsqrt(jnp.maximum(m2, TINY))
    return r, i, log_a, a, a2, m2 * inv_m, inv_m


def gelu_parts(p):
    p2 = p * p
    half = 0.5 * jnp.tanh(p * (GELU_C + (GELU_C * GELU_D) * p2)) + 0.5
    y = p * half
    slope = half + y * (1.0 - half) * (2.0 * GELU_C + (6.0 * GELU_C * GELU_D) * p2)
    return y, slope


def gelu_only(p):
    return p * (0.5 * jnp.tanh(p * (GELU_C + (GELU_C * GELU_D) * (p * p))) + 0.5)


def fill_masks(pos_ref, mask_s):
    pos = pos_ref[...]
    mask_s[0] = jnp.where(pos == 0.0, RESET_LOG, 0.0)
    for k in range(1, CONV_WIDTH):
        mask_s[k] = jnp.where(pos >= float(k), 1.0, 0.0)


def lane_slice(start):
    return pl.ds(pl.multiple_of(start, LANES), LANES)


def row_slice(t, n_seq):
    return pl.ds(pl.multiple_of(t * n_seq, n_seq), n_seq)


def rows_at(t, n_seq):
    return slice(t * n_seq, (t + 1) * n_seq) if isinstance(t, int) else row_slice(t, n_seq)


def conv_lanes(mask_s, vec_ref, xb_ref, c_ref, n_seq, chunks):
    def conv_lane(l, c0):
        col = lane_slice(l * LANES)
        vec = chunk_vec(vec_ref, col)
        old = [xb_ref[l, rows_at(BORROW - k, n_seq), :].astype(F32) for k in range(1, CONV_WIDTH)]
        for t in range(TB):
            r = rows_at(t, n_seq)
            x = xb_ref[l, rows_at(t + BORROW, n_seq), :].astype(F32)
            acc = vec(V_CB) + x * vec(V_CW)
            for k in range(1, CONV_WIDTH):
                acc = acc + (old[k - 1] * mask_s[k, r, :]) * vec(V_CW + k)
            c_ref[l, r, :] = acc.astype(BF16)
            old = [x] + old[:-1]
        return c0

    lax.fori_loop(0, chunks, conv_lane, 0)


def gate_products(wai_ref, c_ref, pa_ref, pi_ref):
    for blk in range(wai_ref.shape[0]):
        pre = dot_nn(c_ref[blk], wai_ref[blk])
        pa_ref[blk] = pre[:, 0:LANES]
        pi_ref[blk] = pre[:, LANES:]


def put_chunks(ref, val, row0):
    for blk in range(ref.shape[0]):
        ref[blk, row0:row0 + val.shape[0], :] = val[:, blk * LANES:(blk + 1) * LANES].astype(ref.dtype)


def local_kernel(x_ref, gz_ref, pos_ref, xh_ref, vec_ref, sc_ref, wx_ref, wy_ref, wo_ref, wai_ref, perm_ref,
                 s_ref, r_ref, info_ref, xt_ref, gt_ref, n_ref, xb_ref, c_ref, py_ref, dm_ref, pa_ref, pi_ref,
                 nt_s, xbt_s, st_s, mask_s):
    n_seq, _, width = x_ref.shape
    own = wx_ref.shape[1]
    chunks = own // LANES
    rows = TB * n_seq
    halo = BORROW * n_seq
    perm = perm_ref[...]

    @pl.when(pl.program_id(0) == 0)
    def _():
        st_s[0] = jnp.zeros(st_s.shape[1:], F32)
        st_s[1] = jnp.ones(st_s.shape[1:], F32)
        st_s[2] = jnp.zeros(st_s.shape[1:], F32)
        for k in range(BORROW):
            nt_s[k * n_seq:(k + 1) * n_seq, :] = norm_rows(xh_ref[k * n_seq:(k + 1) * n_seq, :], sc_ref[0:1, :])
        put_chunks(xbt_s, dot_nn(nt_s[...], wx_ref[...]) + vec_ref[V_BX:V_BX + 1, :], 0)

    to_time_major(perm, x_ref, xt_ref)
    to_time_major(perm, gz_ref, gt_ref)
    n_ref[0, 0:halo, :] = nt_s[...]
    xb_ref[0, :, 0:halo, :] = xbt_s[...]

    fill_masks(pos_ref, mask_s)
    part = 2

    def norm_part(q, c):
        for k in range(part):
            t = q * part + k
            n_ref[0, row_slice(t + BORROW, n_seq), :] = norm_rows(xt_ref[t].astype(F32), sc_ref[0:1, :])
        return c

    lax.fori_loop(0, TB // part, norm_part, 0)
    n_blk = n_ref[0, halo:, :]
    put_chunks(xb_ref.at[0], dot_nn(n_blk, wx_ref[...]) + vec_ref[V_BX:V_BX + 1, :], halo)
    put_chunks(py_ref, dot_nn(n_blk, wy_ref[...]), 0)
    put_chunks(dm_ref, dot_nt(gt_ref[...].reshape(rows, width), wo_ref[...]), 0)
    nt_s[...] = n_ref[0, rows:, :]
    xbt_s[...] = xb_ref[0, :, rows:, :]
    conv_lanes(mask_s, vec_ref, xb_ref.at[0], c_ref, n_seq, chunks)
    gate_products(wai_ref, c_ref, pa_ref, pi_ref)

    def scan_lane(l, c0):
        col = lane_slice(l * LANES)
        vec = chunk_vec(vec_ref, col)

        def scan_t(t, carry):
            h, p, hg = carry
            r = row_slice(t, n_seq)
            _, i, _, a, _, m, _ = gate_terms(pa_ref[l, r, :], pi_ref[l, r, :], vec, mask_s[0, r, :])
            h = a * h + m * i * c_ref[l, r, :].astype(F32)
            p = a * p
            y = gelu_only(py_ref[l, r, :] + vec(V_BY))
            hg = hg + p * (dm_ref[l, r, :] * y)
            return h, p, hg

        h, p, hg = lax.fori_loop(0, TB, scan_t, (st_s[0, :, col], st_s[1, :, col], st_s[2, :, col]), unroll=2)
        st_s[0, :, col] = h
        st_s[1, :, col] = p
        st_s[2, :, col] = hg
        return c0

    lax.fori_loop(0, chunks, scan_lane, 0)
    s_ref[0] = st_s[0]
    r_ref[0] = st_s[1]
    info_ref[...] = st_s[...]


def far_kernel(n_ref, gt_ref, pos_ref, vec_ref, wxy_ref, wo_ref, wai_ref, c_ref, py_ref, dm_ref, pa_ref, pi_ref, xb_s, mask_s):
    n_seq, width = gt_ref.shape[1], gt_ref.shape[2]
    own = wo_ref.shape[0]
    rows = TB * n_seq
    halo = BORROW * n_seq

    @pl.when(pl.program_id(0) == 0)
    def _():
        put_chunks(xb_s, dot_nn(n_ref[0, 0:halo, :], wxy_ref[:, 0:own]) + vec_ref[V_BX:V_BX + 1, :], rows)

    xb_s[:, 0:halo, :] = xb_s[:, rows:, :]
    fill_masks(pos_ref, mask_s)
    n_blk = n_ref[0, halo:, :]
    put_chunks(xb_s, dot_nn(n_blk, wxy_ref[:, 0:own]) + vec_ref[V_BX:V_BX + 1, :], halo)
    put_chunks(py_ref, dot_nn(n_blk, wxy_ref[:, own:]), 0)
    put_chunks(dm_ref, dot_nt(gt_ref[...].reshape(rows, width), wo_ref[...]), 0)
    conv_lanes(mask_s, vec_ref, xb_s, c_ref, n_seq, own // LANES)
    gate_products(wai_ref, c_ref, pa_ref, pi_ref)


def compose_kernel(info_ref, _, out_ref, *, cp_size):
    cp_index = lax.axis_index("cp")
    tp_index = lax.axis_index("tp")
    n_seq, own = info_ref.shape[2], info_ref.shape[3]
    for side in range(2):
        base = jnp.where(side == 0, tp_index, 1 - tp_index) * cp_size
        state = jnp.zeros((n_seq, own), F32)
        grad = jnp.zeros((n_seq, own), F32)
        for q in range(cp_size):
            state = jnp.where(q < cp_index, info_ref[base + q, 1] * state + info_ref[base + q, 0], state)
        for q in range(cp_size - 1, -1, -1):
            grad = jnp.where(q > cp_index, info_ref[base + q, 1] * grad + info_ref[base + q, 2], grad)
        out_ref[0, :, side * own:(side + 1) * own] = state
        out_ref[1, :, side * own:(side + 1) * own] = grad


def norm_back(xf, dn, gain):
    rs = lax.rsqrt(jnp.mean(xf * xf, axis=-1, keepdims=True) + NORM_EPS)
    xh = xf * rs
    dg = dn * xh
    dx = rs * (dn * gain - xh * jnp.mean(dg * gain, axis=-1, keepdims=True))
    return dx, fold8(dg)


def main_kernel(gt_ref, n_ref, xb_ref, pos_ref, c0_ref, c1_ref, py0_ref, py1_ref, dm0_ref, dm1_ref, pa0_ref, pa1_ref, pi0_ref, pi1_ref,
                s0_ref, r0_ref, s1_ref, r1_ref, st_ref, vec_ref, sc_ref, wxy_ref, wai_ref, xh_ref,
                mix_ref, d_ref, gwx_ref, gwy_ref, gwo_ref, gwa_ref, gwi_ref, dxh_ref, gsh_ref,
                dpai_s, g_s, a_s, ka_s, ki_s, k1_s, k3_s, e_s, dh_s, gvec_s, mask_s):
    n_seq, width = gt_ref.shape[1], gt_ref.shape[2]
    chunks = c0_ref.shape[0]
    own = chunks * LANES
    rows = TB * n_seq
    halo = BORROW * n_seq
    step = pl.program_id(0)
    last = step == pl.num_programs(0) - 1

    @pl.when(step == 0)
    def _():
        e_s[...] = jnp.zeros_like(e_s)
        dh_s[...] = st_ref[1]
        for ref in (gwx_ref, gwy_ref, gwo_ref, gwa_ref, gwi_ref, gvec_s):
            ref[...] = jnp.zeros_like(ref)

    fill_masks(pos_ref, mask_s)
    g_rows = gt_ref[...].reshape(rows, width)

    def fwd_lane(side):
        c_ref, py_ref, dm_ref, pa_ref, pi_ref, s_ref, r_ref = ((c0_ref, py0_ref, dm0_ref, pa0_ref, pi0_ref, s0_ref, r0_ref), (c1_ref, py1_ref, dm1_ref, pa1_ref, pi1_ref, s1_ref, r1_ref))[side]

        def run(l, c0):
            loc = lane_slice(l * LANES)
            col = lane_slice(l * LANES + side * own)
            cola = lane_slice(2 * (l * LANES + side * own))
            coli = lane_slice(2 * (l * LANES + side * own) + LANES)
            coly = lane_slice(l * LANES + (2 * side + 1) * own)
            vec = chunk_vec(vec_ref, col)
            state = st_ref[0, :, col]
            state = jnp.where(last, state, s_ref[0, :, loc] + r_ref[0, :, loc] * state)

            h, s_by = state, jnp.zeros((8, LANES), F32)
            for t in range(TB):
                r = rows_at(t, n_seq)
                rg, i, log_a, a, a2, m, inv_m = gate_terms(pa_ref[l, r, :], pi_ref[l, r, :], vec, mask_s[0, r, :])
                cf = c_ref[l, r, :].astype(F32)
                k1 = m * i
                u = k1 * cf
                ah = a * h
                k3r = (ah - (i * cf) * (a2 * inv_m)) * rg
                h = ah + u
                y, slope = gelu_parts(py_ref[l, r, :] + vec(V_BY))
                dm = dm_ref[l, r, :]
                mix_ref[r, col] = (h * y).astype(BF16)
                dpy = dm * h * slope
                d_ref[r, coly] = dpy.astype(BF16)
                g_s[l + side * chunks, r, :] = dm * y
                a_s[l + side * chunks, r, :] = a
                k1_s[l + side * chunks, r, :] = k1
                ka_s[l + side * chunks, r, :] = k3r * (vec(V_SP) - log_a)
                ki_s[l + side * chunks, r, :] = u * (1.0 - i)
                if side == 0:
                    k3_s[l + side * chunks, r, :] = k3r
                    s_by = s_by + fold8(dpy)
            if side == 0:
                gvec_s[S_BY, :, col] += s_by
            return c0

        return run

    lax.fori_loop(0, chunks, fwd_lane(0), 0)
    lax.fori_loop(0, chunks, fwd_lane(1), 0)
    gwo_ref[...] += dot_tn(mix_ref[:, 0:own], g_rows)

    def bwd_lane(side):
        def run(l, c0):
            col = lane_slice(l * LANES + side * own)
            cola = lane_slice(2 * (l * LANES + side * own))
            coli = lane_slice(2 * (l * LANES + side * own) + LANES)

            def body(tt, carry):
                nxt, s_a, s_i, s_p = carry
                r = row_slice(TB - 1 - tt, n_seq)
                dh = g_s[l + side * chunks, r, :] + nxt
                nxt = a_s[l + side * chunks, r, :] * dh
                dpa = dh * ka_s[l + side * chunks, r, :]
                dpi = dh * ki_s[l + side * chunks, r, :]
                g_s[l + side * chunks, r, :] = dh * k1_s[l + side * chunks, r, :]
                dpai_s[l + side * chunks, r, 0:LANES] = dpa.astype(BF16)
                dpai_s[l + side * chunks, r, LANES:] = dpi.astype(BF16)
                if side == 0:
                    s_a = s_a + fold8(dpa)
                    s_i = s_i + fold8(dpi)
                    s_p = s_p + fold8(dh * k3_s[l + side * chunks, r, :])
                return nxt, s_a, s_i, s_p

            zero = jnp.zeros((8, LANES), F32)
            nxt, s_a, s_i, s_p = lax.fori_loop(0, TB, body, (dh_s[:, col], zero, zero, zero), unroll=4)
            dh_s[:, col] = nxt
            if side == 0:
                gvec_s[S_BA, :, col] += s_a
                gvec_s[S_BI, :, col] += s_i
                gvec_s[S_AP, :, col] += s_p
            return c0

        return run

    lax.fori_loop(0, chunks, bwd_lane(0), 0)
    lax.fori_loop(0, chunks, bwd_lane(1), 0)

    for blk in range(2 * chunks):
        g_s[blk] += dot_nt(dpai_s[blk], wai_ref[blk])
        if blk < chunks:
            g_ai = dot_tn(c0_ref[blk], dpai_s[blk])
            gwa_ref[blk] += g_ai[:, 0:LANES]
            gwi_ref[blk] += g_ai[:, LANES:]

    def convb_lane(side):
        def run(l, c0):
            col = lane_slice(l * LANES + side * own)
            colx = lane_slice(l * LANES + 2 * side * own)
            vec = chunk_vec(vec_ref, col)

            e1, e2, e3 = e_s[2 * n_seq:3 * n_seq, col], e_s[n_seq:2 * n_seq, col], e_s[0:n_seq, col]
            s_b = s_x = jnp.zeros((8, LANES), F32)
            taps = [s_b] * CONV_WIDTH
            if side == 0:
                xs = [xb_ref[0, l, rows_at(TB - 1 + BORROW - k, n_seq), :].astype(F32) for k in range(BORROW)]
            dc_next = g_s[l + side * chunks, rows_at(TB - 1, n_seq), :]
            for t in range(TB - 1, -1, -1):
                r = rows_at(t, n_seq)
                dc, dc_next = dc_next, g_s[l + side * chunks, rows_at(max(t - 1, 0), n_seq), :]
                dm = [dc] + [dc * mask_s[k, r, :] for k in range(1, CONV_WIDTH)]
                dx = e1 + dc * vec(V_CW)
                e1 = e2 + dm[1] * vec(V_CW + 1)
                e2 = e3 + dm[2] * vec(V_CW + 2)
                e3 = dm[3] * vec(V_CW + 3)
                d_ref[r, colx] = dx.astype(BF16)
                if side == 0:
                    s_b = s_b + fold8(dc)
                    s_x = s_x + fold8(dx)
                    xs = xs + [xb_ref[0, l, rows_at(t, n_seq), :].astype(F32)]
                    taps = [acc + fold8(dm[k] * xs[k]) for k, acc in enumerate(taps)]
                    xs = xs[1:]
            s0, s1, s2, s3 = taps
            e_s[2 * n_seq:3 * n_seq, col] = e1
            e_s[n_seq:2 * n_seq, col] = e2
            e_s[0:n_seq, col] = e3
            if side == 0:
                for row, val in ((S_CB, s_b), (S_BX, s_x), (S_CW, s0), (S_CW + 1, s1), (S_CW + 2, s2), (S_CW + 3, s3)):
                    gvec_s[row, :, col] += val
            return c0

        return run

    lax.fori_loop(0, chunks, convb_lane(0), 0)
    lax.fori_loop(0, chunks, convb_lane(1), 0)
    n_blk = n_ref[0, halo:, :]
    gwx_ref[...] += dot_tn(n_blk, d_ref[:, 0:own])
    gwy_ref[...] += dot_tn(n_blk, d_ref[:, own:2 * own])

    @pl.when(last)
    def _():
        e16 = e_s[...].astype(BF16)
        gwx_ref[...] += dot_tn(n_ref[0, 0:halo, :], e16[:, 0:own])
        gvec_s[S_BX] += fold8(e_s[0:n_seq, 0:own]) + fold8(e_s[n_seq:2 * n_seq, 0:own]) + fold8(e_s[2 * n_seq:, 0:own])
        dn = dot_nt(e16[:, 0:own], wxy_ref[:, 0:own]) + dot_nt(e16[:, own:], wxy_ref[:, 2 * own:3 * own])
        s_g = jnp.zeros((8, width), F32)
        for k in range(BORROW):
            sl = slice(k * n_seq, (k + 1) * n_seq)
            dx, sg = norm_back(xh_ref[sl, :], dn[sl], sc_ref[0:1, :])
            s_g = s_g + sg
            dxh_ref[sl, :] = dx
        gsh_ref[...] = s_g
        sums = jnp.sum(gvec_s[...], axis=1)
        for q in range(chunks):
            gwa_ref[chunks, q * 16:q * 16 + sums.shape[0], :] = sums[:, q * LANES:(q + 1) * LANES]


def out_kernel(mix_ref, d_ref, xt_ref, gt_ref, fix_ref, gsh_ref, sc_ref, wxy_ref, wo_ref, perm_ref, z_ref, gx_ref, gsc_ref, o_s, q_s, zt_s, gxt_s):
    n_seq, width = xt_ref.shape[1], xt_ref.shape[2]
    rows = TB * n_seq
    halo = BORROW * n_seq
    perm = perm_ref[...]
    step = pl.program_id(0)

    @pl.when(step == 0)
    def _():
        gsc_ref[0] = gsh_ref[...]
        gsc_ref[1] = jnp.zeros((8, width), F32)

    q_s[...] = dot_nt(d_ref[...], wxy_ref[...])
    part = 4

    def gx_part(q, c):
        rp = pl.ds(pl.multiple_of(q * part * n_seq, part * n_seq), part * n_seq)
        o_s[rp, :] = dot_nn(mix_ref[rp, :], wo_ref[...])
        for k in range(part):
            t = q * part + k
            r = row_slice(t, n_seq)
            dx, sg = norm_back(xt_ref[t].astype(F32), q_s[r, :], sc_ref[0:1, :])
            gzf = gt_ref[t].astype(F32)
            gx = gzf + dx
            q_s[r, :] = gx
            gxt_s[t] = gx.astype(BF16)
            gsc_ref[0] += sg
            gsc_ref[1] += fold8(gzf)
        return c

    lax.fori_loop(0, TB // part, gx_part, 0)

    @pl.when(step == pl.num_programs(0) - 1)
    def _():
        tail = q_s[rows - halo:, :] + fix_ref[...]
        gxt_s[TB - BORROW:] = tail.astype(BF16).reshape(BORROW, n_seq, width)

    def z_rows(t, c):
        zt_s[t] = (xt_ref[t].astype(F32) + (o_s[row_slice(t, n_seq), :] + sc_ref[1:2, :])).astype(BF16)
        return c

    lax.fori_loop(0, TB, z_rows, 0, unroll=2)
    to_batch_major(perm, zt_s, z_ref)
    to_batch_major(perm, gxt_s, gx_ref)


def pack_kernel(wx_ref, wy_ref, wo_ref, wa_ref, wi_ref, bx_ref, by_ref, cw_ref, cb_ref, ba_ref, bi_ref, sp_ref, half_ref, vec_ref, wai_ref):
    width, own = wx_ref.shape
    n_blk = wa_ref.shape[0]
    wai_ref[:, :, 0:LANES] = wa_ref[...]
    wai_ref[:, :, LANES:] = wi_ref[...]
    vec_ref[V_BX:V_BX + 1, :] = bx_ref[...].astype(F32).reshape(1, own)
    vec_ref[V_BY:V_BY + 1, :] = by_ref[...].astype(F32).reshape(1, own)
    vec_ref[V_CW:V_CW + CONV_WIDTH, :] = cw_ref[...].astype(F32)
    vec_ref[V_CB:V_CB + 1, :] = cb_ref[...].astype(F32).reshape(1, own)
    vec_ref[V_BA:V_BA + 1, :] = ba_ref[...].astype(F32).reshape(1, own) * (-LOG2E)
    vec_ref[V_BI:V_BI + 1, :] = bi_ref[...].astype(F32).reshape(1, own) * (-LOG2E)
    vec_ref[V_SP:V_SP + 1, :] = sp_ref[...].reshape(1, own)
    vec_ref[V_SP + 1:, :] = jnp.zeros((15 - V_SP, own), F32)
    for side, w_ref in enumerate((wx_ref, wy_ref)):
        @pl.when(lax.rem(lax.axis_index("cp"), 2) == side)
        def _():
            half_ref[0:width, :] = w_ref[...].astype(F32)
            half_ref[width:width + own, :] = wo_ref[:, side * own:(side + 1) * own].astype(F32)
            for k in range(n_blk // 2):
                blk = side * (n_blk // 2) + k
                half_ref[width + own:width + own + LANES, 2 * k * LANES:(2 * k + 1) * LANES] = wa_ref[blk].astype(F32)
                half_ref[width + own:width + own + LANES, (2 * k + 1) * LANES:(2 * k + 2) * LANES] = wi_ref[blk].astype(F32)
            half_ref[width + own + LANES:, :] = vec_ref[side * 8:(side + 1) * 8, :]


def assemble_kernel(wx_ref, wy_ref, wo_ref, wai_ref, vec_ref, mine_ref, other_ref, wxy_out, wo_out, wai_out, vec_out):
    width, own = wx_ref.shape
    n_blk = wai_ref.shape[0]
    wxy_out[:, 0:own] = wx_ref[...]
    wxy_out[:, own:2 * own] = wy_ref[...]
    wo_out[0:own, :] = wo_ref[...]
    wai_out[0:n_blk] = wai_ref[...]
    vec_out[:, 0:own] = vec_ref[...]
    parity = lax.rem(lax.axis_index("cp"), 2)
    for side in range(2):
        for ref, want in ((mine_ref, side), (other_ref, 1 - side)):
            @pl.when(parity == want)
            def _():
                wxy_out[:, (2 + side) * own:(3 + side) * own] = ref[0:width, :].astype(BF16)
                wo_out[own:, side * own:(side + 1) * own] = ref[width:width + own, :].astype(BF16)
                for k in range(n_blk // 2):
                    wai_out[n_blk + side * (n_blk // 2) + k] = ref[width + own:width + own + LANES, 2 * k * LANES:(2 * k + 2) * LANES].astype(BF16)
                vec_out[side * 8:(side + 1) * 8, own:] = ref[width + own + LANES:, :]


def const_spec(shape):
    return pl.BlockSpec(shape, lambda j: (0,) * len(shape), pipeline_mode=pl.Buffered(1))


def shard_body(x_in, grad_z, seg_pos, norm_scale, w_x, b_x, w_y, b_y, conv_w, conv_b, w_a, b_a, w_i, b_i, a_param, w_out, b_out, cp_size):
    n_seq, n_tok, width = x_in.shape
    own = w_x.shape[1]
    full = 2 * own
    nb = n_tok // TB
    rows = TB * n_seq
    halo = BORROW * n_seq
    chunks = own // LANES
    fwd_perm = [(d, d + 1) for d in range(cp_size - 1)]
    back_perm = [(d + 1, d) for d in range(cp_size - 1)]
    swap = [(0, 1), (1, 0)]

    x_tail = x_in[:, n_tok - BORROW:, :].astype(F32).transpose(1, 0, 2).reshape(halo, width)
    x_halo = lax.ppermute(x_tail, "cp", fwd_perm)

    sp8 = -8.0 * jax.nn.softplus(a_param)
    half, vec_own, w_ai = pl.pallas_call(
        pack_kernel,
        out_shape=[jax.ShapeDtypeStruct((width + own + LANES + 8, own), F32), jax.ShapeDtypeStruct((16, own), F32), jax.ShapeDtypeStruct((chunks, LANES, 2 * LANES), BF16)],
        compiler_params=pltpu.CompilerParams(vmem_limit_bytes=VMEM_BYTES),
        name="pack",
    )(w_x, w_y, w_out, w_a, w_i, b_x, b_y, conv_w, conv_b, b_a, b_i, sp8)
    far_half = lax.ppermute(half, "tp", swap)
    far_other = lax.ppermute(far_half, "cp", [(d, d ^ 1) for d in range(cp_size)])

    pos = jnp.broadcast_to(seg_pos.T.astype(F32).reshape(n_tok * n_seq, 1), (n_tok * n_seq, LANES))
    scales = jnp.concatenate([1.0 + norm_scale.astype(F32)[None], b_out.astype(F32)[None], jnp.zeros((6, width), F32)], axis=0)
    line = np.arange(TB * TB)
    perm = jnp.asarray((line[:, None] // TB == line[None, :] % TB) & (line[:, None] % TB == line[None, :] // TB), BF16)

    def vmem(shape, dtype):
        return pltpu.VMEM(shape, dtype)

    def sds(shape, dtype):
        return jax.ShapeDtypeStruct(shape, dtype)

    params = pltpu.CompilerParams(vmem_limit_bytes=VMEM_BYTES, dimension_semantics=("arbitrary",))

    def cost(gflop):
        return pl.CostEstimate(flops=gflop * 10 ** 9, bytes_accessed=10 ** 8, transcendentals=0)

    def blocks(idx):
        batch = pl.BlockSpec((n_seq, TB, width), lambda j: (0, idx(j), 0))
        time = pl.BlockSpec((TB, n_seq, width), lambda j: (idx(j), 0, 0))
        row = lambda cols: pl.BlockSpec((rows, cols), lambda j: (idx(j), 0))
        per = lambda *dims: pl.BlockSpec((1,) + dims, lambda j: (idx(j), 0, 0))
        chk = pl.BlockSpec((chunks, rows, LANES), lambda j: (0, idx(j), 0))
        xbs = pl.BlockSpec((1, chunks, rows + halo, LANES), lambda j: (idx(j), 0, 0, 0))
        return batch, time, row, per, chk, xbs

    batch, time, row, per, chk, xbs = blocks(lambda j: j)
    tok = n_tok * n_seq
    ends, prods, info, xt, gt, n_all, xb, c_own, py_own, dm_own, pa_own, pi_own = pl.pallas_call(
        local_kernel,
        grid=(nb,),
        in_specs=[batch, batch, row(LANES), const_spec((halo, width)), const_spec((16, own)), const_spec((8, width)),
                  const_spec((width, own)), const_spec((width, own)), const_spec((own, width)), const_spec(w_ai.shape), const_spec(perm.shape)],
        out_specs=[per(n_seq, own), per(n_seq, own), const_spec((3, n_seq, own)), time, time, per(rows + halo, width), xbs,
                   chk, chk, chk, chk, chk],
        out_shape=[sds((nb, n_seq, own), F32), sds((nb, n_seq, own), F32), sds((3, n_seq, own), F32), sds((n_tok, n_seq, width), BF16), sds((n_tok, n_seq, width), BF16),
                   sds((nb, rows + halo, width), BF16), sds((nb, chunks, rows + halo, LANES), BF16), sds((chunks, tok, LANES), BF16)] + [sds((chunks, tok, LANES), F32)] * 4,
        scratch_shapes=[vmem((halo, width), BF16), vmem((chunks, halo, LANES), BF16), vmem((3, n_seq, own), F32), vmem((CONV_WIDTH, rows, LANES), F32)],
        compiler_params=params, cost_estimate=cost(100), name="local_pass",
    )(x_in, grad_z, pos, x_halo, vec_own, scales, w_x, w_y, w_out, w_ai, perm)

    infos = lax.all_gather(info, ("tp", "cp"))
    far_ends = lax.ppermute(ends, "tp", swap)
    far_prods = lax.ppermute(prods, "tp", swap)

    w_xy, w_o, w_g, vec = pl.pallas_call(
        assemble_kernel,
        out_shape=[sds((width, 4 * own), BF16), sds((full, width), BF16), sds((2 * chunks,) + w_ai.shape[1:], BF16), sds((16, full), F32)],
        compiler_params=pltpu.CompilerParams(vmem_limit_bytes=VMEM_BYTES),
        name="assemble",
    )(w_x, w_y, w_out, w_ai, vec_own, far_half, far_other)

    c_far, py_far, dm_far, pa_far, pi_far = pl.pallas_call(
        far_kernel,
        grid=(nb,),
        in_specs=[per(rows + halo, width), time, row(LANES), pl.BlockSpec((16, own), lambda j: (0, 1), pipeline_mode=pl.Buffered(1)),
                  pl.BlockSpec((width, full), lambda j: (0, 1), pipeline_mode=pl.Buffered(1)), pl.BlockSpec((own, width), lambda j: (1, 0), pipeline_mode=pl.Buffered(1)),
                  pl.BlockSpec(w_ai.shape, lambda j: (1, 0, 0), pipeline_mode=pl.Buffered(1))],
        out_specs=[chk] * 5,
        out_shape=[sds((chunks, tok, LANES), BF16)] + [sds((chunks, tok, LANES), F32)] * 4,
        scratch_shapes=[vmem((chunks, rows + halo, LANES), BF16), vmem((CONV_WIDTH, rows, LANES), F32)],
        compiler_params=params, cost_estimate=cost(50), name="far_pass",
    )(n_all, gt, pos, vec, w_xy, w_o, w_g)

    states = pl.pallas_call(
        functools.partial(compose_kernel, cp_size=cp_size),
        in_specs=[pl.BlockSpec(memory_space=pltpu.VMEM), pl.BlockSpec(memory_space=pl.ANY)],
        out_shape=sds((2, n_seq, full), F32),
        compiler_params=pltpu.CompilerParams(vmem_limit_bytes=VMEM_BYTES),
        name="compose",
    )(infos, c_far)

    batch, time, row, per, chk, xbs = blocks(lambda j: nb - 1 - j)
    bound = pl.BlockSpec((1, n_seq, own), lambda j: (jnp.maximum(nb - 2 - j, 0), 0, 0))
    mix, d_all, g_wx, g_wy, g_wo, g_wa, g_wi, dx_halo, g_sh = pl.pallas_call(
        main_kernel,
        grid=(nb,),
        in_specs=[time, per(rows + halo, width), xbs, row(LANES)] + [chk] * 10 + [
                  bound, bound, bound, bound, const_spec((2, n_seq, full)), const_spec((16, full)), const_spec((8, width)),
                  const_spec((width, 2 * full)), const_spec(w_g.shape), const_spec((halo, width))],
        out_specs=[row(full), row(2 * full), const_spec((width, own)), const_spec((width, own)), const_spec((own, width)),
                   const_spec((chunks + 1, LANES, LANES)), const_spec((chunks, LANES, LANES)), const_spec((halo, width)), const_spec((8, width))],
        out_shape=[sds((tok, full), BF16), sds((tok, 2 * full), BF16), sds((width, own), F32), sds((width, own), F32), sds((own, width), F32),
                   sds((chunks + 1, LANES, LANES), F32), sds((chunks, LANES, LANES), F32), sds((halo, width), F32), sds((8, width), F32)],
        scratch_shapes=[vmem((2 * chunks, rows, 2 * LANES), BF16)] + [vmem((2 * chunks, rows, LANES), F32)] * 5 + [vmem((chunks, rows, LANES), F32), vmem((halo, full), F32), vmem((n_seq, full), F32), vmem((10, 8, own), F32), vmem((CONV_WIDTH, rows, LANES), F32)],
        compiler_params=params, cost_estimate=cost(300), name="main_pass",
    )(gt, n_all, xb, pos, c_own, c_far, py_own, py_far, dm_own, dm_far, pa_own, pa_far, pi_own, pi_far, ends, prods, far_ends, far_prods, states, vec, scales, w_xy, w_g, x_halo)

    fix = lax.ppermute(dx_halo, "cp", back_perm)
    g_wx, g_wy, g_wo, g_wa, g_wi = lax.psum((g_wx, g_wy, g_wo, g_wa, g_wi), "cp")

    batch, time, row, per, chk, xbs = blocks(lambda j: j)
    z_out, grad_x, g_sc = pl.pallas_call(
        out_kernel,
        grid=(nb,),
        in_specs=[row(full), row(2 * full), time, time, const_spec((halo, width)), const_spec((8, width)), const_spec((8, width)),
                  const_spec((width, 2 * full)), const_spec((full, width)), const_spec(perm.shape)],
        out_specs=[batch, batch, const_spec((2, 8, width))],
        out_shape=[sds(x_in.shape, BF16), sds(x_in.shape, BF16), sds((2, 8, width), F32)],
        scratch_shapes=[vmem((rows, width), F32), vmem((rows, width), F32), vmem((TB, n_seq, width), BF16), vmem((TB, n_seq, width), BF16)],
        compiler_params=params, cost_estimate=cost(100), name="out_pass",
    )(mix, d_all, xt, gt, fix, g_sh, scales, w_xy, w_o, perm)

    g_sc = jnp.sum(g_sc, axis=1)
    hop = 1
    while hop < cp_size:
        g_sc = g_sc + lax.ppermute(g_sc, "cp", [(d, d ^ hop) for d in range(cp_size)])
        hop *= 2

    sums = jnp.concatenate([g_wa[chunks, q * 16:q * 16 + 10, :] for q in range(chunks)], axis=1)
    g_ap = sums[S_AP] * (-8.0) * jax.nn.sigmoid(a_param)
    return (z_out, grad_x, g_sc[0], g_wx, sums[S_BX], g_wy, sums[S_BY], sums[S_CW:S_CW + 4],
            sums[S_CB], g_wa[:chunks], sums[S_BA], g_wi, sums[S_BI], g_ap, g_wo, g_sc[1])


def solution(mesh):
    per_device = functools.partial(shard_body, cp_size=mesh.shape["cp"])
    return jax.shard_map(per_device, mesh=mesh, in_specs=IN_SPECS, out_specs=OUT_SPECS, check_vma=False)
```

time: 4690 us -> 586 us (0.12); the launches traced: 4630 us -> 585 us
  local copies, waits for them, and re-layouts: 1890 us -> 16.8 us
  waiting for transfers between devices: 1420 us -> 76.3 us
  other arithmetic: 1020 us -> 7.92 us
  Pallas kernels: 0 us -> 451 us
  matrix products: 240 us -> 0 us
    psum x2 -> x1, waiting for transfers between devices: 1400 us -> 0.01 us  [shard_body(): lax.psum((g_wx, g_wy, g_wo, g_wa, g_wi), 'cp')]
    dynamic_update_slice x1040 -> x0, local copies, waits for them, and re-layouts: 1130 us -> none  [the longest x1024 1120 us: local_scan(): lax.scan(scan_step, (zeros_h, jnp.ones_like(zeros_h)), (decays, drives))]
    dynamic_slice x513 -> x0, local copies, waits for them, and re-layouts: 559 us -> none  [the longest x512 559 us: local_scan(): lax.scan(scan_step, (zeros_h, jnp.ones_like(zeros_h)), (decays, drives))]
    pallas_call x0 -> x7, Pallas kernels: none -> 451 us  [the longest x1 170 us: shard_body(): pl.pallas_call(main_kernel, grid=(nb,), in_specs=[time, per(rows + halo,...]
    dynamic_update_slice x264 -> x0, other arithmetic: 394 us -> none  [the longest x256 394 us: local_scan(): lax.scan(scan_step, (zeros_h, jnp.ones_like(zeros_h)), (decays, drives))]
    reduce_sum x10 -> x1, other arithmetic: 254 us -> 0.87 us  [shard_body(): g_sc = jnp.sum(g_sc, axis=1)]
    mul x258 -> x3, other arithmetic: 255 us -> 2.47 us  [the longest x1 1.28 us: shard_body(): sp8 = -8.0 * jax.nn.softplus(a_param)]
    dot_general x15 -> x0, matrix products: 240 us -> none  [the longest x1 28 us: shard_body(): jnp.einsum('btd,ld->tbl', grad_z, w_out, preferred_element_type=jnp.float32)]
  transfers between devices with their start and end apart: 6 -> 11, of which waited for: 3 -> 5; matrix products, arithmetic and copies ran while one was open for 7% -> 1% of each run, Pallas kernels for 0% -> 47%
where the time goes in v1:
time: 586 us; the launch traced here: 585 us
  Pallas kernels  451 us (77%)
  waiting for transfers between devices  76.3 us (13%)
  starting transfers between devices  18.7 us (3%)
  local copies, waits for them, and re-layouts  16.8 us (3%)
  between operations  14.1 us (2%)
  other arithmetic  7.92 us (1%)
    pallas_call x1, Pallas kernels, shard_body(): pl.pallas_call(main_kernel, grid=(nb,), in_specs=[time, per(rows + halo,...  170 us
    pallas_call x1, Pallas kernels, shard_body(): pl.pallas_call(local_kernel, grid=(nb,), in_specs=[batch, batch, row(LANE...  109 us
    pallas_call x1, Pallas kernels, shard_body(): pl.pallas_call(out_kernel, grid=(nb,), in_specs=[row(full), row(2 * full)...  103 us
    ppermute x1, waiting for transfers between devices, shard_body(): far_half = lax.ppermute(half, 'tp', swap)  68.4 us
    pallas_call x1, Pallas kernels, shard_body(): pl.pallas_call(far_kernel, grid=(nb,), in_specs=[per(rows + halo, width),...  54.3 us
  transfers between devices with their start and end apart: 11, of which 5 were waited for; matrix products, arithmetic and copies ran while one was open for 1% of the time, Pallas kernels for 47%

profile of v1, /device:TPU:0, one launch (start us, length us, event | category | flops | bytes accessed | tf_op | source)
XLA Modules:
  0.0 584.5 jit_solution(3642638171588949148)
XLA Ops:
  7.2 1.3 fusion.sp_ref
  8.5 4.1 pack.1
  12.6 3.3 collective-permute-start.1
  17.3 1.5 collective-permute-start
  21.9 68.4 %collective-permute-done.1.mine_ref = f32[1672,512]{1,0:T(8,128)} collective-permute-done((f32[1672,512]{1,0:T(8,128)}, f32[1672,512]{1,0:T(8,128)}, u32[]{:S(2)}, u32[]{:S(2)}) %collective-permute-start.1) | collective-permute-done | bytes 3424288 | tf_op jit(solution)/shard_map/ppermute | solution.py:548
  90.3 2.6 broadcast_in_dim.18.pos_ref
  92.9 108.8 %local_pass.1 = (f32[16,32,512]{2,1,0:T(8,128)}, f32[16,32,512]{2,1,0:T(8,128)}, f32[3,32,512]{2,1,0:T(8,128)}, bf16[256,32,1024]{2,1,0:T(8,128)(2,1)}, bf16[256...) custom-call(bf16[32,256,1024]{2,1,0:T(8,128)(2,1)} %x_ref.1, ...), custom_call_target="tpu_custom_call" | custom-call | flops 99999997952 | bytes 100000000 | tf_op jit(solution)/shard_map/local_pass/pallas_call | solution.py:578
  201.8 1.8 collective-permute-start.3
  203.8 7.7 %assemble.1 = (bf16[1024,2048]{1,0:T(8,128)(2,1)}, bf16[1024,1024]{1,0:T(8,128)(2,1)}, bf16[8,128,256]{2,1,0:T(8,128)(2,1)}, f32[16,1024]{1,0:T(8,128)}) custom-call(bf16[1024,512]{1,0:T(8,128)(2,1)} %wx_ref.5, bf16[1024,512]{1,0:T(8,128)(2,1)} %wy_ref.5, bf16[512,1024]{1,0:T(8,128)(2,1)} %wo_ref.5, bf16[4,128,256]{2,1,0:T(8,128)(2,1)} %get-tuple-element.53.wai_ref, ...), custom_call_target="tpu_custom_call" | custom-call | tf_op jit(solution)/shard_map/assemble/pallas_call | solution.py:595
  211.5 54.3 %far_pass.1 = (bf16[4,8192,128]{2,1,0:T(8,128)(2,1)}, f32[4,8192,128]{2,1,0:T(8,128)}, f32[4,8192,128]{2,1,0:T(8,128)}, f32[4,8192,128]{2,1,0:T(8,128)}, f32[4,8192,128]{2,1,0:T(8,128)}) custom-call(bf16[16,608,1024]{2,1,0:T(8,128)(2,1)} %get-tuple-element.55.n_ref, bf16[256,32,1024]{2,1,0:T(8,128)(2,1)} %get-tuple-element.54.gt_ref, ...), custom_call_target="tpu_custom_call" | custom-call | flops 49999998976 | bytes 100000000 | tf_op jit(solution)/shard_map/far_pass/pallas_call | solution.py:602
  265.8 2.8 compose.1.st_ref
  268.6 169.9 %main_pass.1 = (bf16[8192,1024]{1,0:T(8,128)(2,1)}, bf16[8192,2048]{1,0:T(8,128)(2,1)}, f32[1024,512]{1,0:T(8,128)}, f32[1024,512]{1,0:T(8,128)}, f32[512,1024]{...) custom-call(bf16[256,32,1024]{2,1,0:T(8,128)(2,1)} %get-tuple-element.54, ...), custom_call_target="tpu_custom_call" | custom-call | flops 299999985664 | bytes 100000000 | tf_op jit(solution)/shard_map/main_pass/pallas_call | solution.py:624
  438.5 1.3 collective-permute-start.5
  439.8 2.5 collective-permute-done.5.fix_ref
  443.1 103.1 %out_pass.1 = (bf16[32,256,1024]{2,1,0:T(8,128)(2,1)}, bf16[32,256,1024]{2,1,0:T(8,128)(2,1)}, f32[2,8,1024]{2,1,0:T(8,128)}) custom-call(bf16[8192,1024]{1,0:T(8,128)(2,1)} %get-tuple-element.75.mix_ref, bf16[8192,2048]{1,0:T(8,128)(2,1)} %get-tuple-element.76.d_ref, bf16[256,32,1024]{2,1,0:T(8,128)(2,1)} %get-tuple-element.77.xt_ref, ...), custom_call_target="tpu_custom_call" | custom-call | flops 99999997952 | bytes 100000000 | tf_op jit(solution)/shard_map/out_pass/pallas_call | solution.py:642
  547.1 5.8 collective-permute-start.6
  553.7 4.0 collective-permute-start.7
  557.7 1.6 collective-permute-done.7
  560.1 2.9 collective-permute-done.8
  564.5 1.7 slice.66
  568.5 3.1 copy.44
  571.6 3.1 copy.45
  574.7 1.7 copy.46
  576.3 1.3 copy.47
  (43 shorter events, 12.0 us)
Async XLA Ops:
  7.2 258.6 %all-gather.3.cloned.1.call-start = ((), (), s32[]{:S(2)}) async-start(), calls=%async_computation | async-start | bytes 3342336 | tf_op jit(solution)/shard_map/all_gather | solution.py:591
  12.6 77.7 %collective-permute-start.1 = (f32[1672,512]{1,0:T(8,128)}, f32[1672,512]{1,0:T(8,128)}, u32[]{:S(2)}, u32[]{:S(2)}) collective-permute-start(f32[1672,512]{1,0:T(8,128)} %get-tuple-element.58), channel_id=1, source_target_pairs={{0,8},{8,0},{1,9},{9,1},{2,10},{10,2},{3,11},{11,3},{4,12},{12,4},... | collective-permute-start | bytes 10272776 | tf_op jit(solution)/shard_map/ppermute | solution.py:548
  17.3 73.0 %collective-permute-start = (f32[96,1024]{1,0:T(8,128)S(1)}, f32[96,1024]{1,0:T(8,128)S(1)}, u32[]{:S(2)}, u32[]{:S(2)}) collective-permute-start(f32[96,1024]{1,0:T(8,128)S(1)} %bitcast.25), channel_id=1, source_target_pairs={{0,1},{1,2},{2,3},{3,4},{4,5},{5,6},{6,7},{8,9},{9,10},{10,11},{11... | collective-permute-start | bytes 1179656 | tf_op jit(solution)/shard_map/ppermute | solution.py:539
  90.3 113.6 %collective-permute-start.2 = (f32[1672,512]{1,0:T(8,128)}, f32[1672,512]{1,0:T(8,128)}, u32[]{:S(2)}, u32[]{:S(2)}) collective-permute-start(f32[1672,512]{1,0:T(8,128)} %collective-permute-done.1.mine_ref), channel_id=1, source_target_pairs={{0,1},{1,0},{2,3},{3,2},{4,5},{5,4},{6,7},{7,6},{8,9},{9,8},{10,11... | collective-permute-start | bytes 10272776 | tf_op jit(solution)/shard_map/ppermute | solution.py:549
  90.3 2.6 copy-start.2
  201.7 361.8 %all-reduce.3.cloned.1.call-start = ((), (), s32[]{:S(2)}) async-start(), calls=%async_computation.1 | async-start | bytes 13762560 | tf_op jit(solution)/shard_map/psum | solution.py:639
  201.8 66.8 %collective-permute-start.3 = (f32[16,32,512]{2,1,0:T(8,128)}, f32[16,32,512]{2,1,0:T(8,128)}, u32[]{:S(2)}, u32[]{:S(2)}) collective-permute-start(f32[16,32,512]{2,1,0:T(8,128)} %get-tuple-element.72.s0_ref), channel_id=1, source_target_pairs={{0,8},{8,0},{1,9},{9,1},{2,10},{10,2},{3,11},{11,3},{4,12},{12,4},... | collective-permute-start | bytes 3145736 | tf_op jit(solution)/shard_map/ppermute | solution.py:592
  203.6 65.1 %collective-permute-start.4 = (f32[16,32,512]{2,1,0:T(8,128)}, f32[16,32,512]{2,1,0:T(8,128)}, u32[]{:S(2)}, u32[]{:S(2)}) collective-permute-start(f32[16,32,512]{2,1,0:T(8,128)} %get-tuple-element.73.r0_ref), channel_id=1, source_target_pairs={{0,8},{8,0},{1,9},{9,1},{2,10},{10,2},{3,11},{11,3},{4,12},{12,4},... | collective-permute-start | bytes 3145736 | tf_op jit(solution)/shard_map/ppermute | solution.py:593
  438.5 3.8 collective-permute-start.5
  442.3 0.8 copy-start.3
  443.1 124.8 %copy-start.1 = (f32[512]{0:T(512)S(1)}, f32[512]{0:T(512)}, u32[]{:S(2)}) copy-start(f32[512]{0:T(512)} %param.32) | copy-start | bytes 6148
  547.1 6.6 %collective-permute-start.6 = (f32[2,1024]{1,0:T(2,128)S(1)}, f32[2,1024]{1,0:T(2,128)S(1)}, u32[]{:S(2)}, u32[]{:S(2)}) collective-permute-start(f32[2,1024]{1,0:T(2,128)S(1)} %reduce_sum.9), channel_id=1, source_target_pairs={{0,1},{1,0},{2,3},{3,2},{4,5},{5,4},{6,7},{7,6},{8,9},{9,8},{10,11... | collective-permute-start | bytes 24584 | tf_op jit(solution)/shard_map/ppermute | solution.py:656
  553.7 5.6 collective-permute-start.7
  559.3 3.7 collective-permute-start.8
  563.6 12.8 %copy-start = (f32[512,1024]{1,0:T(8,128)S(1)}, f32[512,1024]{1,0:T(8,128)}, u32[]{:S(2)}) copy-start(f32[512,1024]{1,0:T(8,128)} %get-tuple-element.119) | copy-start | bytes 6291460
Sparse Core Ops, SparseCore 0:
  201.8 43.3 all-gather.2
  440.0 106.8 all-reduce.2
